TPU v7x, 512 devices: a whole 4x4x16 slice. The times are simulated.
512 devices in a mesh: verts: 128 (over z, y, core), modes: 4 (over x).
Axes of the slice: x: 4, y: 4, z: 16, core: 2. Of those that a mesh axis runs over, the one named last changes fastest.
Arguments:
- reduced_coords: float32 [256], P('modes'), may hold values from -4 to 4
- mode_basis: bfloat16 [256, 3, 131072], P('modes', None, 'verts'), may hold values from -0.375 to 0.375
- rest_shape: float32 [3, 131072], P(None, 'verts'), may hold values from -6 to 6
- stiffness: float32 [131072], P('verts'), may hold values from 0.2 to 2
- send_slots: int32 [128, 128, 16], P('verts'), may hold values from 0 to 1023
- pair_peer: int32 [128, 2, 1024], P('verts'), may hold values from 0 to 127
- pair_slot: int32 [128, 2, 1024], P('verts'), may hold values from 0 to 15
- pair_count: int32 [128], P('verts'), may hold values from 1 to 1024, 65536 in all
Outputs:
- hessian: float32 [256, 256], P('modes')
- gradient: float32 [256], P('modes')
Inputs may be any that keep to these rules, and one draw needn't show every extreme that they name: `send_slots`: indices may repeat. `pair_count`: the counts sum to 128 * 512 and the busiest owner has all 1024 slots live; slots at and beyond an owner's count hold valid but unused indices.
All inputs are finite; a program needn't handle non-finite values. No bound on the sum of `pair_count` on one device may be relied on, other than what follows from the above.
Results may differ from a plain program's by a relative error of at most 0.0046.
Values may be sent and summed in bfloat16 or wider, within the bound.
A program may use at most 64 MiB of HBM per device.

v0:
```python
import jax
import jax.numpy as jnp
from jax import lax
from jax.sharding import Mesh
from jax.sharding import PartitionSpec as P

VERTS = ("verts_0", "verts_1", "verts_2")


highest = lax.Precision.HIGHEST
barrier_reach = 1.5
gap_offset = 0.1


def sent_to_all(x, axis):
    size = lax.axis_size(axis)
    return lax.all_to_all(jnp.broadcast_to(x[None], (size, *x.shape)), axis, 0, 0, tiled=True)


def over_copies(x, axis):
    return sent_to_all(x, axis).sum(axis=0)


def in_order(tiles, dim):
    tiles = jnp.moveaxis(tiles, 0, dim)
    dims = tiles.shape
    return tiles.reshape(*dims[:dim], dims[dim] * dims[dim + 1], *dims[dim + 2 :])


def collect(x, axis, dim):
    return in_order(sent_to_all(x, axis), dim)


def split_up(x, dim, size):
    dims = x.shape
    tiles = x.reshape(*dims[:dim], size, dims[dim] // size, *dims[dim + 1 :])
    return jnp.moveaxis(tiles, dim, 0)


def sum_at_owner(x, axis, dim):
    tiles = split_up(x, dim, lax.axis_size(axis))
    arrived = lax.all_to_all(tiles, axis, split_axis=0, concat_axis=0, tiled=True)
    return arrived.sum(axis=0)


def sum_by_axis(x, axes, dim):
    far, near = axes
    own = sum_at_owner(split_up(x, dim, lax.axis_size(far)), near, dim + 1)
    return jnp.sum(lax.all_to_all(own, far, 0, 0, tiled=True), axis=0)


def padded_to(lines, size):
    spare = -len(lines) % size
    return jnp.pad(lines, [(0, spare)] + [(0, 0)] * (lines.ndim - 1))


def gather_axes(x, axes, dim):
    far, near = axes
    first = sent_to_all(x, far)
    tiles = jnp.swapaxes(sent_to_all(first, near), 0, 1)
    return in_order(tiles.reshape(-1, *x.shape), dim)


def sum_by_parts(x, axes):
    own = sum_by_axis(padded_to(x, lax.axis_size(axes[0]) * lax.axis_size(axes[1])), axes, 0)
    whole = gather_axes(own, axes, 0)
    return whole[: len(x)].reshape(x.shape)


def together(arrays, axis):
    ends = [0]
    for a in arrays:
        ends.append(ends[-1] + a.size)
    subtotal = sum_by_parts(jnp.concatenate([a.ravel() for a in arrays]), axis)
    return tuple((subtotal[b:e].reshape(a.shape) for a, b, e in zip(arrays, ends, ends[1:])))


def barrier_slopes(distance):
    excess = distance - barrier_reach
    ratio_log = jnp.log(distance / barrier_reach)
    slope_term = -(2.0 * excess * ratio_log + excess * excess / distance)
    curvature = -(
        2.0 * ratio_log + 4.0 * excess / distance - excess * excess / (distance * distance)
    )
    inside = distance < barrier_reach
    return (jnp.where(inside, slope_term, 0.0), jnp.where(inside, curvature, 0.0))


def outer_sum(left_rows, right_rows):
    return lax.dot_general(
        left_rows, right_rows, (((1,), (1,)), ((), ())), preferred_element_type=jnp.float32
    )


def spring_terms(displacement, stiffness):
    radius = jnp.sqrt(1.0 + jnp.sum(displacement * displacement, axis=0))
    spring_rate = stiffness / radius
    return (spring_rate, -spring_rate / (radius * radius), spring_rate * displacement)


def elastic_left(basis_block, displacement, spring_rate, curvature_rate):
    mode_count, _, vertex_count = basis_block.shape
    projected = jnp.sum(basis_block * displacement[None], axis=1)
    scaled = (spring_rate * basis_block).astype(jnp.bfloat16)
    return jnp.concatenate(
        [
            scaled.reshape(mode_count, 3 * vertex_count),
            (curvature_rate * projected).astype(jnp.bfloat16),
        ],
        axis=1,
    )


def elastic_right(basis_block, displacement):
    mode_count, _, vertex_count = basis_block.shape
    projected = jnp.sum(basis_block * displacement[None], axis=1)
    return jnp.concatenate(
        [basis_block.reshape(mode_count, 3 * vertex_count), projected.astype(jnp.bfloat16)], axis=1
    )


def contact_terms(rows_first, rows_second, separation, active):
    mode_count, _, slot_total = rows_first.shape
    distance = jnp.sum(separation * separation, axis=0) + gap_offset
    slope_term, curvature = barrier_slopes(distance)
    slope_term = slope_term * active
    curvature = curvature * active
    difference = rows_first.astype(jnp.float32) - rows_second.astype(jnp.float32)
    leverage = jnp.sum(difference * separation[None], axis=1)
    left_rows = jnp.concatenate(
        [
            (2.0 * slope_term * difference)
            .astype(jnp.bfloat16)
            .reshape(mode_count, 3 * slot_total),
            (4.0 * curvature * leverage).astype(jnp.bfloat16),
        ],
        axis=1,
    )
    right_rows = jnp.concatenate(
        [
            difference.astype(jnp.bfloat16).reshape(mode_count, 3 * slot_total),
            leverage.astype(jnp.bfloat16),
        ],
        axis=1,
    )
    contact_grad = jnp.sum(difference * (2.0 * slope_term * separation)[None], axis=(1, 2))
    return (left_rows, right_rows, contact_grad)


def body(
    reduced_coords, mode_basis, rest_shape, stiffness, send_slots, pair_peer, pair_slot, pair_count
):
    local_modes, _, vertex_count = mode_basis.shape
    peer_count = lax.axis_size(VERTS)
    mode_groups = lax.axis_size("modes")
    mode_count = local_modes * mode_groups
    factor = mode_count / (3.0 * vertex_count * peer_count)
    partial_value = jnp.dot(
        reduced_coords,
        mode_basis.reshape(local_modes, 3 * vertex_count),
        precision=highest,
        preferred_element_type=jnp.float32,
    ).reshape(3, vertex_count)
    positions = rest_shape + over_copies(partial_value, "modes")
    displacement = positions - rest_shape
    spring_rate, curvature_rate, elastic_force = spring_terms(displacement, stiffness)
    send_ids = send_slots[0]
    slot_count = send_ids.shape[1]
    flat_slots = send_ids.reshape(-1)
    outgoing_pos = jnp.take(positions, flat_slots, axis=1).reshape(3, peer_count, slot_count)
    outgoing_rows = jnp.take(mode_basis, flat_slots, axis=2).reshape(
        local_modes, 3, peer_count, slot_count
    )
    incoming_pos = lax.all_to_all(outgoing_pos, VERTS, split_axis=1, concat_axis=1, tiled=True)
    incoming_rows = lax.all_to_all(outgoing_rows, VERTS, split_axis=2, concat_axis=2, tiled=True)
    slot_total = pair_peer.shape[2]
    endpoints = (pair_peer[0] * slot_count + pair_slot[0]).reshape(-1)
    pos_ends = jnp.take(
        incoming_pos.reshape(3, peer_count * slot_count), endpoints, axis=1
    ).reshape(3, 2, slot_total)
    row_ends = jnp.take(
        incoming_rows.reshape(local_modes, 3, peer_count * slot_count), endpoints, axis=2
    ).reshape(local_modes, 3, 2, slot_total)
    separation = pos_ends[:, 0] - pos_ends[:, 1]
    active = (jnp.arange(slot_total, dtype=jnp.int32) < pair_count[0]).astype(jnp.float32)
    contact_left, contact_right, contact_grad = contact_terms(
        row_ends[:, :, 0], row_ends[:, :, 1], separation, active
    )
    left_rows = elastic_left(mode_basis, displacement, spring_rate, curvature_rate)
    hessian = outer_sum(left_rows, elastic_right(collect(mode_basis, "modes", 0), displacement))
    hessian = hessian + outer_sum(contact_left, collect(contact_right, "modes", 0))
    elastic_grad = jnp.dot(
        mode_basis.reshape(local_modes, 3 * vertex_count),
        elastic_force.reshape(3 * vertex_count),
        precision=highest,
        preferred_element_type=jnp.float32,
    )
    hessian, gradient = together(
        (hessian, elastic_grad + contact_grad), (("verts_0", "verts_1"), "verts_2")
    )
    return (hessian * factor, gradient * factor)


def solution(mesh):
    finer = Mesh(
        mesh.devices.reshape(16, 4, 2, mesh.shape["modes"]),
        ("verts_0", "verts_1", "verts_2", "modes"),
    )
    placed = (
        P("modes"),
        P("modes", None, VERTS),
        P(None, VERTS),
        P(VERTS),
        P(VERTS, None, None),
        P(VERTS, None, None),
        P(VERTS, None, None),
        P(VERTS),
    )
    return jax.shard_map(
        body, mesh=finer, in_specs=placed, out_specs=(P("modes", None), P("modes")), check_vma=False
    )
```

profile of v0, /device:TPU:1, one launch (start us, length us, event | category | flops | bytes accessed | tf_op | source)
XLA Modules:
  0.0 260.3 jit_solution(9859768531721757224)
XLA Ops:
  1.3 1.3 fusion.23
  3.2 4.8 %all-to-all-start = ((f32[4,3,1024]{2,1,0:T(4,128)}), f32[4,3,1024]{2,1,0:T(4,128)S(1)}, u32[]{:S(2)}, u32[]{:S(2)}) async-start(f32[4,3,1024]{2,1,0:T(4,128)} %broadcast_in_dim.86), calls=%async_computation | async-start | bytes 131072 | tf_op jit(solution)/shard_map/all_to_all | solution.py:17
  9.7 1.6 copy.131
  11.4 14.6 %gather_fusion.2 = bf16[2048,64,3]{1,2,0:T(4,128)(2,1)} fusion(bf16[64,3,1024]{0,1,2:T(4,128)(2,1)S(1)} %copy.131, s32[2048]{0:T(1024)S(1)} %broadcast_clamp_fusion.1), kind=kCustom, calls=%fused_computation.2 | custom fusion | bytes 1581056 | tf_op jit(solution)/shard_map/jit(_take)/gather | solution.py:171
  26.0 1.8 copy.132
  27.9 1.2 multiply_reduce_fusion.2
  29.3 5.5 %gather_fusion = f32[2048,3]{1,0:T(8,128)S(1)} fusion(f32[3,1024]{0,1:T(8,128)S(1)} %copy.126, s32[2048]{0:T(1024)S(1)} %broadcast_clamp_fusion.1), kind=kCustom, calls=%fused_computation | custom fusion | bytes 57344 | tf_op jit(solution)/shard_map/jit(_take)/gather | solution.py:170
  36.4 20.5 %all-to-all-start.2 = ((f32[3,128,16]{2,0,1:T(4,128)}), f32[3,128,16]{2,0,1:T(4,128)}, u32[]{:S(2)}, u32[]{:S(2)}) async-start(f32[3,128,16]{2,0,1:T(4,128)} %broadcast_select_fusion.2), calls=%async_computation.2 | async-start | bytes 524288 | tf_op jit(solution)/shard_map/all_to_all | solution.py:174
  57.6 1.8 reshape.296
  59.3 17.6 %all-to-all-done.2 = f32[3,128,16]{2,0,1:T(4,128)} async-done(((f32[3,128,16]{2,0,1:T(4,128)}), f32[3,128,16]{2,0,1:T(4,128)}, u32[]{:S(2)}, u32[]{:S(2)}) %all-to-all-start.2) | async-done | bytes 24608 | tf_op jit(solution)/shard_map/all_to_all | solution.py:174
  77.0 8.3 %all-to-all-start.3 = ((bf16[128,2,1536]{2,1,0:T(2,128)(2,1)}), bf16[128,2,1536]{2,1,0:T(2,128)(2,1)S(1)}, u32[]{:S(2)}, u32[]{:S(2)}) async-start(bf16[128,2,1536]{2,1,0:T(2,128)(2,1)} %reshape.296), calls=%async_computation.3 | async-start | bytes 1572864 | tf_op jit(solution)/shard_map/all_to_all | solution.py:175
  88.3 1.8 copy.128
  90.1 5.5 %gather_fusion.1 = f32[2048,3]{1,0:T(8,128)S(1)} fusion(f32[3,2048]{0,1:T(8,128)S(1)} %bitcast.98, s32[2048]{0:T(1024)S(1)} %broadcast_clamp_fusion), kind=kCustom, calls=%fused_computation.1 | custom fusion | bytes 57344 | tf_op jit(solution)/shard_map/jit(_take)/gather | solution.py:178
  97.2 29.8 %all-to-all-done.3 = bf16[128,2,1536]{2,1,0:T(2,128)(2,1)S(1)} async-done(((bf16[128,2,1536]{2,1,0:T(2,128)(2,1)}), bf16[128,2,1536]{2,1,0:T(2,128)(2,1)S(1)}, u32[]{:S(2)}, u32[]{:S(2)}) %all-to-all-start.3) | async-done | bytes 786464 | tf_op jit(solution)/shard_map/all_to_all | solution.py:175
  127.0 1.4 broadcast_in_dim.87
  128.4 4.5 %all-to-all-start.1 = ((bf16[4,64,3,1024]{3,1,2,0:T(8,128)(2,1)}), bf16[4,64,3,1024]{3,1,2,0:T(8,128)(2,1)S(1)}, u32[]{:S(2)}, u32[]{:S(2)}) async-start(bf16[4,64,3,1024]{3,1,2,0:T(8,128)(2,1)} %broadcast_in_dim.87), calls=%async_computation.1 | async-start | bytes 3145728 | tf_op jit(solution)/shard_map/all_to_all | solution.py:17
  132.9 2.9 %reshape.297 = bf16[128,3,16,64]{3,2,1,0:T(8,128)(2,1)S(1)} reshape(bf16[128,2,1536]{2,1,0:T(2,128)(2,1)} %copy-done.2) | data formatting | bytes 1572864
  136.1 10.7 %copy.135 = bf16[64,3,2048]{0,1,2:T(4,128)(2,1)} copy(bf16[64,3,2048]{0,2,1:T(8,128)(2,1)S(1)} %bitcast.94) | data formatting | bytes 1572864 | tf_op jit(solution)/shard_map/reshape | solution.py:182
  146.9 16.1 %gather_fusion.3 = bf16[2048,64,3]{1,2,0:T(4,128)(2,1)} fusion(bf16[64,3,2048]{0,1,2:T(4,128)(2,1)} %copy.135, s32[2048]{0:T(1024)S(1)} %broadcast_clamp_fusion), kind=kCustom, calls=%fused_computation.3 | custom fusion | bytes 1581056 | tf_op jit(solution)/shard_map/jit(_take)/gather | solution.py:181
  162.9 3.4 %copy.136 = bf16[64,3,2,1024]{3,1,0,2:T(4,128)(2,1)S(1)} copy(bf16[64,3,2,1024]{0,1,3,2:T(4,128)(2,1)} %bitcast.95) | data formatting | bytes 1572864 | tf_op jit(solution)/shard_map/jit(_take)/gather | solution.py:181
  167.6 1.6 fusion.11
  170.0 1.6 broadcast_in_dim.97
  171.6 4.8 %all-to-all-start.4 = ((bf16[4,64,4096]{2,1,0:T(8,128)(2,1)}), bf16[4,64,4096]{2,1,0:T(8,128)(2,1)}, u32[]{:S(2)}, u32[]{:S(2)}) async-start(bf16[4,64,4096]{2,1,0:T(8,128)(2,1)} %broadcast_in_dim.97), calls=%async_computation.4 | async-start | bytes 4194304 | tf_op jit(solution)/shard_map/all_to_all | solution.py:17
  177.2 1.4 copy.123
  178.5 1.9 copy.147
  182.7 18.4 %all-to-all-done.4 = bf16[4,64,4096]{2,1,0:T(8,128)(2,1)} async-done(((bf16[4,64,4096]{2,1,0:T(8,128)(2,1)}), bf16[4,64,4096]{2,1,0:T(8,128)(2,1)}, u32[]{:S(2)}, u32[]{:S(2)}) %all-to-all-start.4) | async-done | bytes 2097184 | tf_op jit(solution)/shard_map/all_to_all | solution.py:17
  201.0 2.4 fusion.18
  203.5 1.8 fusion.7
  205.8 6.3 %all_to_all.50 = f32[2,64,129]{2,1,0:T(8,128)S(1)} all-to-all(f32[2,64,129]{2,1,0:T(8,128)S(1)} %copy.137), channel_id=1, replica_groups=mesh['verts_0'=16,'verts_1'=4,'verts_2'=2,'modes'=4] {'verts_2'}, dimensions={0} | all-to-all | bytes 132096 | tf_op jit(solution)/shard_map/all_to_all | solution.py:42
  212.1 21.9 %all_to_all.51 = f32[64,1,129]{2,1,0:T(1,128)S(1)} all-to-all(f32[64,1,129]{2,1,0:T(1,128)S(1)} %all_to_all.37), channel_id=1, replica_groups=mesh['verts_0'=16,'verts_1'=4,'verts_2'=2,'modes'=4] {'verts_0','verts_1'}, dimensions={0} | all-to-all | bytes 66048 | tf_op jit(solution)/shard_map/all_to_all | solution.py:49
  234.2 18.5 %all_to_all.52 = f32[64,1,129]{2,1,0:T(1,128)S(1)} all-to-all(f32[64,1,129]{2,1,0:T(1,128)S(1)} %broadcast_in_dim.98), channel_id=1, replica_groups=mesh['verts_0'=16,'verts_1'=4,'verts_2'=2,'modes'=4] {'verts_0','verts_1'}, dimensions={0} | all-to-all | bytes 66048 | tf_op jit(solution)/shard_map/all_to_all | solution.py:17
  252.7 6.0 %all_to_all.53 = f32[2,64,129]{2,1,0:T(8,128)S(1)} all-to-all(f32[2,64,129]{2,1,0:T(8,128)S(1)} %broadcast_in_dim.100), channel_id=1, replica_groups=mesh['verts_0'=16,'verts_1'=4,'verts_2'=2,'modes'=4] {'verts_2'}, dimensions={0} | all-to-all | bytes 132096 | tf_op jit(solution)/shard_map/all_to_all | solution.py:17
  (105 shorter events, 17.0 us)
Async XLA Ops:
  0.6 0.7 copy-start
  3.2 24.6 %all-to-all-start = ((f32[4,3,1024]{2,1,0:T(4,128)}), f32[4,3,1024]{2,1,0:T(4,128)S(1)}, u32[]{:S(2)}, u32[]{:S(2)}) async-start(f32[4,3,1024]{2,1,0:T(4,128)} %broadcast_in_dim.86), calls=%async_computation | async-start | bytes 131072 | tf_op jit(solution)/shard_map/all_to_all | solution.py:17
  26.0 1.9 copy-start.20
  36.4 40.6 %all-to-all-start.2 = ((f32[3,128,16]{2,0,1:T(4,128)}), f32[3,128,16]{2,0,1:T(4,128)}, u32[]{:S(2)}, u32[]{:S(2)}) async-start(f32[3,128,16]{2,0,1:T(4,128)} %broadcast_select_fusion.2), calls=%async_computation.2 | async-start | bytes 524288 | tf_op jit(solution)/shard_map/all_to_all | solution.py:174
  57.5 27.8 %copy-start.16 = (s32[1,2,1024]{2,1,0:T(2,128)S(1)}, s32[1,2,1024]{2,1,0:T(2,128)}, u32[]{:S(2)}) copy-start(s32[1,2,1024]{2,1,0:T(2,128)} %param.14) | copy-start | bytes 24580
  57.5 27.8 %copy-start.17 = (s32[1,2,1024]{2,1,0:T(2,128)S(1)}, s32[1,2,1024]{2,1,0:T(2,128)}, u32[]{:S(2)}) copy-start(s32[1,2,1024]{2,1,0:T(2,128)} %param.13) | copy-start | bytes 24580
  57.5 28.5 %copy-start.21 = (f32[1024]{0:T(1024)S(1)}, f32[1024]{0:T(1024)}, u32[]{:S(2)}) copy-start(f32[1024]{0:T(1024)} %get-tuple-element.4) | copy-start | bytes 12292
  57.5 28.5 %copy-start.22 = (f32[1024]{0:T(1024)S(1)}, f32[1024]{0:T(1024)}, u32[]{:S(2)}) copy-start(f32[1024]{0:T(1024)} %param.11) | copy-start | bytes 12292
  57.5 29.2 %copy-start.1 = (bf16[64,3,1024]{2,0,1:T(8,128)(2,1)S(1)}, bf16[64,3,1024]{2,0,1:T(8,128)(2,1)}, u32[]{:S(2)}) copy-start(bf16[64,3,1024]{2,0,1:T(8,128)(2,1)} %param.9) | copy-start | bytes 1179652
  57.5 29.1 %copy-start.6 = (f32[3,1024]{1,0:T(4,128)S(1)}, f32[3,1024]{1,0:T(4,128)}, u32[]{:S(2)}) copy-start(f32[3,1024]{1,0:T(4,128)} %get-tuple-element.5) | copy-start | bytes 36868
  77.0 50.0 %all-to-all-start.3 = ((bf16[128,2,1536]{2,1,0:T(2,128)(2,1)}), bf16[128,2,1536]{2,1,0:T(2,128)(2,1)S(1)}, u32[]{:S(2)}, u32[]{:S(2)}) async-start(bf16[128,2,1536]{2,1,0:T(2,128)(2,1)} %reshape.296), calls=%async_computation.3 | async-start | bytes 1572864 | tf_op jit(solution)/shard_map/all_to_all | solution.py:175
  86.7 0.9 copy-start.12
  96.0 32.4 %copy-start.8 = (f32[3,1024]{1,0:T(4,128)}, f32[3,1024]{1,0:T(4,128)S(1)}, u32[]{:S(2)}) copy-start(f32[3,1024]{1,0:T(4,128)S(1)} %get-tuple-element.8) | copy-start | bytes 36868
  96.6 31.8 %copy-start.14 = (f32[1024]{0:T(1024)}, f32[1024]{0:T(1024)S(1)}, u32[]{:S(2)}) copy-start(f32[1024]{0:T(1024)S(1)} %get-tuple-element.16) | copy-start | bytes 12292
  127.0 1.4 copy-start.2
  128.4 41.6 %all-to-all-start.1 = ((bf16[4,64,3,1024]{3,1,2,0:T(8,128)(2,1)}), bf16[4,64,3,1024]{3,1,2,0:T(8,128)(2,1)S(1)}, u32[]{:S(2)}, u32[]{:S(2)}) async-start(bf16[4,64,3,1024]{3,1,2,0:T(8,128)(2,1)} %broadcast_in_dim.87), calls=%async_computation.1 | async-start | bytes 3145728 | tf_op jit(solution)/shard_map/all_to_all | solution.py:17
  166.8 0.8 copy-start.9
  166.8 0.8 copy-start.11
  167.1 2.2 copy-start.18
  171.6 4.8 %copy-start.7 = (f32[3,1024]{1,0:T(4,128)S(1)}, f32[3,1024]{1,0:T(4,128)}, u32[]{:S(2)}) copy-start(f32[3,1024]{1,0:T(4,128)} %get-tuple-element.5) | copy-start | bytes 36868
  171.6 4.8 %copy-start.13 = (f32[1024]{0:T(1024)S(1)}, f32[1024]{0:T(1024)}, u32[]{:S(2)}) copy-start(f32[1024]{0:T(1024)} %copy-done.12) | copy-start | bytes 12292
  171.6 4.9 %copy-start.4 = (f32[64,1024]{1,0:T(8,128)S(1)}, f32[64,1024]{1,0:T(8,128)}, u32[]{:S(2)}) copy-start(f32[64,1024]{1,0:T(8,128)} %get-tuple-element.10) | copy-start | bytes 786436
  171.6 4.9 %copy-start.19 = (f32[1024]{0:T(1024)S(1)}, f32[1024]{0:T(1024)}, u32[]{:S(2)}) copy-start(f32[1024]{0:T(1024)} %get-tuple-element.13) | copy-start | bytes 12292
  171.6 5.5 %copy-start.15 = (f32[1024]{0:T(1024)S(1)}, f32[1024]{0:T(1024)}, u32[]{:S(2)}) copy-start(f32[1024]{0:T(1024)} %copy-done.14) | copy-start | bytes 12292
  171.6 29.4 %all-to-all-start.4 = ((bf16[4,64,4096]{2,1,0:T(8,128)(2,1)}), bf16[4,64,4096]{2,1,0:T(8,128)(2,1)}, u32[]{:S(2)}, u32[]{:S(2)}) async-start(bf16[4,64,4096]{2,1,0:T(8,128)(2,1)} %broadcast_in_dim.97), calls=%async_computation.4 | async-start | bytes 4194304 | tf_op jit(solution)/shard_map/all_to_all | solution.py:17
  181.7 21.8 %copy-start.3 = (bf16[32,8,3,1024]{3,1,2,0:T(8,128)(2,1)S(1)}, bf16[32,8,3,1024]{3,1,2,0:T(8,128)(2,1)}, u32[]{:S(2)}) copy-start(bf16[32,8,3,1024]{3,1,2,0:T(8,128)(2,1)} %copy.147) | copy-start | bytes 4718596
  182.6 20.9 %copy-start.5 = (bf16[4,64,1024]{2,1,0:T(8,128)(2,1)S(1)}, bf16[4,64,1024]{2,1,0:T(8,128)(2,1)}, u32[]{:S(2)}) copy-start(bf16[4,64,1024]{2,1,0:T(8,128)(2,1)} %multiply_reduce_fusion) | copy-start | bytes 1572868
  182.6 20.9 %copy-start.10 = (bf16[64,1024]{1,0:T(8,128)(2,1)S(1)}, bf16[64,1024]{1,0:T(8,128)(2,1)}, u32[]{:S(2)}) copy-start(bf16[64,1024]{1,0:T(8,128)(2,1)} %multiply_convert_fusion.2) | copy-start | bytes 393220
  203.5 1.8 copy-start.23
where the time goes:
time: 261 us; the launch traced here: 260 us
  local copies, waits for them, and re-layouts  78.9 us (30%)
  waiting for transfers between devices  65.8 us (25%)
  blocking collectives  52.7 us (20%)
  starting transfers between devices  42.9 us (16%)
  other arithmetic  11.8 us (5%)
  matrix products  6.41 us (2%)
    all_to_all x1, waiting for transfers between devices, body(): lax.all_to_all(outgoing_rows, VERTS, split_axis=2, concat_axis=2, tiled=T...  29.8 us
    all_to_all x2, blocking collectives, sent_to_all(): lax.all_to_all(jnp.broadcast_to(x[None], (size, *x.shape)), axis, 0, 0, t...  24.5 us
    all_to_all x1, blocking collectives, sum_by_axis(): return jnp.sum(lax.all_to_all(own, far, 0, 0, tiled=True), axis=0)  21.9 us
    all_to_all x1, starting transfers between devices, body(): lax.all_to_all(outgoing_pos, VERTS, split_axis=1, concat_axis=1, tiled=True)  20.5 us
    gather x2, local copies, waits for them, and re-layouts, body(): jnp.take(incoming_rows.reshape(local_modes, 3, peer_count * slot_count),...  19.5 us
    all_to_all x3, waiting for transfers between devices, sent_to_all(): lax.all_to_all(jnp.broadcast_to(x[None], (size, *x.shape)), axis, 0, 0, t...  18.4 us
    all_to_all x1, waiting for transfers between devices, body(): lax.all_to_all(outgoing_pos, VERTS, split_axis=1, concat_axis=1, tiled=True)  17.6 us
    gather x2, local copies, waits for them, and re-layouts, body(): jnp.take(mode_basis, flat_slots, axis=2)  16.4 us
  transfers between devices with their start and end apart: 5, of which 3 were waited for; matrix products, arithmetic and copies ran while one was open for 29% of the time, Pallas kernels for 0%

commit v1 on v0

v1 whole, which is shorter than its diff:
```python
import jax
import jax.numpy as jnp
from jax import lax
from jax.experimental import pallas as pl
from jax.experimental.pallas import tpu as pltpu
from jax.sharding import Mesh
from jax.sharding import PartitionSpec as P

VERTS = ("z", "y", "c")
MESH = pl.DeviceIdType.MESH
NZ, NS, NX = 16, 8, 4
NP = NX * NS
LM, LC = 64, 192
NV, NPAIR, NSLOT = 1024, 1024, 16
Q = 256
ROWS = 24
GROUP = 4
f32, bf16 = jnp.float32, jnp.bfloat16

barrier_reach = 1.5
gap_offset = 0.1


def split3(v):
    hi = v.astype(bf16).astype(f32)
    mid = (v - hi).astype(bf16).astype(f32)
    return hi, mid, v - hi - mid


def dot_nt(a, b):
    return lax.dot_general(a, b, (((1,), (1,)), ((), ())), preferred_element_type=f32)


def dot_nn(a, b):
    return lax.dot_general(a, b, (((1,), (0,)), ((), ())), preferred_element_type=f32)


def offset_of(n):
    half = n // 2
    return 8 + half - (n % 2) * (2 * half + 1)


def barrier_slopes(distance):
    excess = distance - barrier_reach
    ratio_log = jnp.log(distance / barrier_reach)
    slope_term = -(2.0 * excess * ratio_log + excess * excess / distance)
    curvature = -(2.0 * ratio_log + 4.0 * excess / distance - excess * excess / (distance * distance))
    inside = distance < barrier_reach
    return jnp.where(inside, slope_term, 0.0), jnp.where(inside, curvature, 0.0)


def accumulate(rows_ref, s, scale, bend, hess, grad, first):
    rows = rows_ref[...]
    lever = jnp.zeros((NX * LM, Q), f32)
    total = None
    slopes = None
    for k in range(3):
        xb = rows[:, LM * k : LM * (k + 1), :].reshape(NX * LM, Q)
        x = xb.astype(f32)
        sk = s[k : k + 1, :]
        lever = lever + x * sk
        part = dot_nt((x * scale).astype(bf16), xb)
        total = part if total is None else total + part
        hi, mid, lo = split3(scale * sk)
        force = jnp.concatenate([hi, mid, lo, jnp.zeros((13, Q), f32)], axis=0).astype(bf16)
        gpart = dot_nt(force, xb)
        slopes = gpart if slopes is None else slopes + gpart
    total = total + dot_nt((lever * bend).astype(bf16), lever.astype(bf16))
    slopes = jnp.sum(slopes, axis=0, keepdims=True)
    if first:
        hess[...] = total
        grad[...] = slopes
    else:
        hess[...] = hess[...] + total
        grad[...] = grad[...] + slopes


def kernel(
    factor,
    basis_ref, coeff_ref, rest_ref, stiff_ref, slots_ref, ends_ref, count_ref,
    out_h, out_g,
    wide, obuf, stage, rows_in, restg, restp, resta, restz,
    part_s, xb, xp, acc, dsend, usend, xd, xu,
    hess, grad, hsend, hplane, zsend, hz, csend, hc,
    p1_s, p1_r, ri_s, ri_r, rz_s, rz_r, zm_s, zm_r,
    x_s, x_r, a_s, a_r, b_s, b_r, c_s, c_r,
):
    z, y, c, x = (lax.axis_index(n) for n in ("z", "y", "c", "x"))
    s = y * 2 + c
    p = x * NS + s

    def place(xq, sq):
        return {"x": xq, "y": sq // 2, "c": lax.rem(sq, 2)}

    def plane_peer(k):
        q = lax.rem(p + k, NP)
        return q, place(q // NS, lax.rem(q, NS))

    def near_peer(k):
        q = lax.rem(s + k, NS)
        return q, {"y": q // 2, "c": lax.rem(q, 2)}

    def remote(src, dst, ssem, rsem, where):
        return pltpu.make_async_remote_copy(src, dst, ssem, rsem, device_id=where, device_id_type=MESH)

    bar = pltpu.get_barrier_semaphore()

    @pl.loop(1, NZ)
    def _(k):
        pl.semaphore_signal(bar, inc=1, device_id={"z": lax.rem(z + k, NZ)}, device_id_type=MESH)

    @pl.loop(1, NP)
    def _(k):
        pl.semaphore_signal(bar, inc=1, device_id=plane_peer(k)[1], device_id_type=MESH)

    wide[0:LC, :] = basis_ref[...]
    wide[LC:Q, :] = jnp.zeros((Q - LC, NV), bf16)
    rest = rest_ref[...]
    mine = jnp.where(x == 0, rest[0:1], jnp.where(x == 1, rest[1:2], jnp.where(x == 2, rest[2:3], 0.0)))
    hi, mid, lo = split3(mine)
    rest_rows = jnp.concatenate([hi, mid, lo, jnp.zeros((13, NV), f32)], axis=0).astype(bf16)
    lane = lax.broadcasted_iota(jnp.int32, (128, 128), 1).astype(f32)

    @pl.loop(0, NZ // GROUP)
    def _(g):
        hots = []
        for i in range(GROUP):
            zq = lax.rem(z + offset_of(g * GROUP + i), NZ)
            row = slots_ref[pl.ds(zq, 1), :].astype(f32)
            col = jnp.transpose(jnp.broadcast_to(row, (128, 128)))
            blocks = [jnp.where(col == lane + 128.0 * b, 1.0, 0.0).astype(bf16) for b in range(NV // 128)]
            hots.append(jnp.concatenate(blocks, axis=1))
        hot = jnp.concatenate(hots, axis=0)
        picked = dot_nt(hot, wide[...])
        tail = picked[:, 128:256]
        turned = pltpu.roll(tail, 64, 1)
        tail = tail.reshape(GROUP * NS, 2, 8, 128)[:, 0] + turned.reshape(GROUP * NS, 2, 8, 128)[:, 1]
        chunk = jnp.concatenate([picked[:, 0:128].reshape(GROUP * NS, 16, 128), tail], axis=1)
        chunk = chunk.astype(bf16).reshape(GROUP, NS, ROWS, 128)
        rests = jnp.sum(dot_nt(rest_rows, hot), axis=0, keepdims=True)
        for i in range(GROUP):
            n = g * GROUP + i
            obuf[:, pl.ds(n, 1)] = chunk[i][:, None]
            restg[pl.ds(n, 1), :] = rests[:, 128 * i : 128 * (i + 1)]

    coeff = coeff_ref[...]
    moved = dot_nn(coeff, basis_ref[...])
    part_s[...] = moved[0:8] + moved[8:16] + moved[16:24]

    pl.semaphore_wait(bar, NZ - 1 + NP - 1)

    for g in range(NZ // GROUP):
        span = pl.ds(g * GROUP, GROUP)

        @pl.loop(1, NS)
        def _(k):
            q, where = near_peer(k)
            remote(obuf.at[q, span], stage.at[span, s], p1_s.at[g], p1_r.at[g], where).start()

    @pl.loop(1, NS)
    def _(k):
        _q, where = near_peer(k)
        remote(restg, restp.at[s], ri_s, ri_r, where).start()

    @pl.loop(1, NX)
    def _(k):
        q = lax.rem(x + k, NX)
        cols = pl.ds(pl.multiple_of(q * Q, Q), Q)
        remote(basis_ref.at[:, cols], xb.at[x], x_s.at[0], x_r.at[0], {"x": q}).start()
        remote(part_s.at[:, cols], xp.at[x], x_s.at[1], x_r.at[1], {"x": q}).start()

    own = pl.ds(pl.multiple_of(x * Q, Q), Q)
    xb[x] = basis_ref[:, own]
    xp[x] = part_s[:, own]
    stage[:, pl.ds(s, 1)] = obuf[s][:, None]
    restp[s] = restg[...]

    for g in range(NZ // GROUP):
        whole = obuf.at[pl.ds(0, NS - 1), pl.ds(0, GROUP)]
        remote(whole, whole, p1_s.at[g], p1_r.at[g], {"z": z}).wait_recv()
        for i in range(GROUP):
            n = g * GROUP + i
            if n < NZ - 1:
                remote(stage.at[n], rows_in.at[n], zm_s, zm_r.at[n], {"z": lax.rem(z + offset_of(n), NZ)}).start()
        if g == 0:
            remote(restp.at[pl.ds(0, NS - 1)], restp.at[pl.ds(0, NS - 1)], ri_s, ri_r, {"z": z}).wait_recv()
            place_of = lax.broadcasted_iota(jnp.int32, (NZ, 128), 1) // NSLOT
            gathered = jnp.zeros((NZ, 128), f32)
            for q in range(NS):
                shift = lax.rem((q - s + NS) * NSLOT, 128)
                gathered = jnp.where(place_of == q, pltpu.roll(restp[q], shift, 1), gathered)
            resta[...] = gathered.reshape(NZ, 1, 128)
            for n in range(NZ - 1):
                remote(resta.at[n], restz.at[n], rz_s, rz_r, {"z": lax.rem(z + offset_of(n), NZ)}).start()
            restz[NZ - 1] = resta[NZ - 1]
    rows_in[NZ - 1] = stage[NZ - 1]

    for i, buf in ((0, xb), (1, xp)):
        remote(buf.at[pl.ds(0, NX - 1)], buf.at[pl.ds(0, NX - 1)], x_s.at[i], x_r.at[i], {"z": z}).wait_recv()
    disp = xp[0] + xp[1] + xp[2] + xp[3]
    square = 1.0 + disp[0:1] * disp[0:1] + disp[1:2] * disp[1:2] + disp[2:3] * disp[2:3]
    rate = stiff_ref[:, own] / jnp.sqrt(square)
    accumulate(xb, disp, rate, -rate / square, hess, grad, True)

    acc[...] = jnp.zeros_like(acc)
    remote(resta.at[pl.ds(0, NZ - 1)], restz.at[pl.ds(0, NZ - 1)], rz_s, rz_r, {"z": z}).wait_recv()
    pick = lax.broadcasted_iota(jnp.int32, (8, 128), 0) == x
    code = lax.broadcasted_iota(jnp.int32, (128, NPAIR), 0)

    def absorb(n):
        base = lax.rem(z + NZ - offset_of(n), NZ) * 128
        first = jnp.where(ends_ref[0:1, :] - base == code, 1.0, 0.0)
        second = jnp.where(ends_ref[1:2, :] - base == code, 1.0, 0.0)
        return (first - second).astype(bf16)

    def consume(n, choose):
        got = rows_in[n].astype(f32)
        head = got[:, 0:16].reshape(128, 128)
        tail = got[:, 16:24]
        turned = pltpu.roll(tail.reshape(64, 128), 64, 1).reshape(NS, 1, 8, 128)
        tail = jnp.concatenate([tail.reshape(NS, 1, 8, 128), turned], axis=1).reshape(128, 128)
        cols = jnp.concatenate([jnp.transpose(head), jnp.transpose(tail)[0:LM]], axis=0).astype(bf16)
        pos = dot_nn(coeff, cols)
        pos = pos[0:8] + pos[8:16] + pos[16:24] + jnp.where(pick, restz[n], 0.0)
        hi, mid, lo = split3(pos)
        pos = jnp.concatenate([hi, mid, lo, jnp.zeros((8, 128), f32)], axis=0).astype(bf16)
        acc[...] = acc[...] + dot_nn(jnp.concatenate([cols, pos], axis=0), choose)

    consume(NZ - 1, absorb(NZ - 1))

    @pl.loop(0, NZ - 1)
    def _(n):
        choose = absorb(n)
        remote(stage.at[n], rows_in.at[n], zm_s, zm_r.at[n], {"z": z}).wait_recv()
        consume(n, choose)

    dsend[...] = acc[0:LC, :].astype(bf16)
    usend[...] = acc[LC : LC + 8, :] + acc[LC + 8 : LC + 16, :] + acc[LC + 16 : LC + 24, :]

    @pl.loop(1, NX)
    def _(k):
        q = lax.rem(x + k, NX)
        cols = pl.ds(pl.multiple_of(q * Q, Q), Q)
        remote(usend.at[:, cols], xu.at[x], x_s.at[3], x_r.at[3], {"x": q}).start()
        remote(dsend.at[:, cols], xd.at[x], x_s.at[2], x_r.at[2], {"x": q}).start()

    xd[x] = dsend[:, own]
    xu[x] = usend[:, own]
    remote(xu.at[pl.ds(0, NX - 1)], xu.at[pl.ds(0, NX - 1)], x_s.at[3], x_r.at[3], {"z": z}).wait_recv()
    gap = xu[0] + xu[1] + xu[2] + xu[3]
    distance = gap[0:1] * gap[0:1] + gap[1:2] * gap[1:2] + gap[2:3] * gap[2:3] + gap_offset
    slope, bend = barrier_slopes(distance)
    live = lax.broadcasted_iota(jnp.int32, (1, Q), 1) + x * Q < count_ref[0]
    slope = jnp.where(live, slope, 0.0)
    bend = jnp.where(live, bend, 0.0)
    remote(xd.at[pl.ds(0, NX - 1)], xd.at[pl.ds(0, NX - 1)], x_s.at[2], x_r.at[2], {"z": z}).wait_recv()
    accumulate(xd, gap, 2.0 * slope, 4.0 * bend, hess, grad, False)

    def packed_grad(row):
        hi = row.astype(bf16).astype(f32)
        lo = row - hi
        return jnp.concatenate(
            [hi[:, 0:128], hi[:, 128:256], lo[:, 0:128], lo[:, 128:256], jnp.zeros((4, 128), f32)], axis=0
        )

    h = hess[...]
    tail = jnp.broadcast_to(packed_grad(grad[...])[None], (NP, 8, 128))
    hsend[...] = jnp.concatenate(
        [h[:, 0:128].reshape(NP, 8, 128), h[:, 128:256].reshape(NP, 8, 128), tail], axis=1
    ).astype(bf16)

    @pl.loop(1, NP)
    def _(k):
        q, where = plane_peer(k)
        remote(hsend.at[q], hplane.at[p], a_s, a_r, where).start()

    hplane[p] = hsend[p]
    remote(hsend.at[pl.ds(0, NP - 1)], hplane.at[pl.ds(0, NP - 1)], a_s, a_r, {"z": z}).wait_recv()
    total = jnp.sum(hplane[...].astype(f32), axis=0)
    g0, g1 = total[16:17] + total[18:19], total[17:18] + total[19:20]
    zsend[...] = jnp.concatenate([total[0:16], packed_grad(jnp.concatenate([g0, g1], axis=1))], axis=0).astype(bf16)

    @pl.loop(1, NZ)
    def _(k):
        remote(zsend, hz.at[z], b_s, b_r, {"z": lax.rem(z + k, NZ)}).start()

    hz[z] = zsend[...]
    remote(hz.at[pl.ds(0, NZ - 1)], hz.at[pl.ds(0, NZ - 1)], b_s, b_r, {"z": z}).wait_recv()
    total = jnp.sum(hz[...].astype(f32), axis=0) * factor
    csend[...] = total[0:16]

    @pl.loop(1, NS)
    def _(k):
        _q, where = near_peer(k)
        remote(csend, hc.at[s], c_s, c_r, where).start()

    hc[s] = csend[...]
    g0, g1 = total[16:17] + total[18:19], total[17:18] + total[19:20]
    half = jnp.where(x >= 2, g1, g0)
    half = jnp.where(lax.rem(x, 2) == 1, pltpu.roll(jnp.broadcast_to(half, (8, 128)), 64, 1), half)
    out_g[...] = half
    remote(hc.at[pl.ds(0, NS - 1)], hc.at[pl.ds(0, NS - 1)], c_s, c_r, {"z": z}).wait_recv()
    out_h[:, 0:128] = hc[:, 0:8, :].reshape(LM, 128)
    out_h[:, 128:256] = hc[:, 8:16, :].reshape(LM, 128)

    for g in range(NZ // GROUP):
        whole = obuf.at[pl.ds(0, NS - 1), pl.ds(0, GROUP)]
        remote(whole, whole, p1_s.at[g], p1_r.at[g], {"z": z}).wait_send()
    for src, sem in (
        (restp.at[pl.ds(0, NS - 1)], ri_s),
        (resta.at[pl.ds(0, NZ - 1)], rz_s),
        (stage.at[pl.ds(0, NZ - 1)], zm_s),
        (xb.at[pl.ds(0, NX - 1)], x_s.at[0]),
        (xp.at[pl.ds(0, NX - 1)], x_s.at[1]),
        (xd.at[pl.ds(0, NX - 1)], x_s.at[2]),
        (xu.at[pl.ds(0, NX - 1)], x_s.at[3]),
        (hsend.at[pl.ds(0, NP - 1)], a_s),
        (hz.at[pl.ds(0, NZ - 1)], b_s),
        (hc.at[pl.ds(0, NS - 1)], c_s),
    ):
        remote(src, src, sem, c_r, {"z": z}).wait_send()


def step(factor, *operands):
    dma = pltpu.SemaphoreType.DMA
    scratch = [
        pltpu.VMEM((Q, NV), bf16),
        pltpu.VMEM((NS, NZ, ROWS, 128), bf16),
        pltpu.VMEM((NZ, NS, ROWS, 128), bf16),
        pltpu.VMEM((NZ, NS, ROWS, 128), bf16),
        pltpu.VMEM((NZ, 128), f32),
        pltpu.VMEM((NS, NZ, 128), f32),
        pltpu.VMEM((NZ, 1, 128), f32),
        pltpu.VMEM((NZ, 1, 128), f32),
        pltpu.VMEM((8, NV), f32),
        pltpu.VMEM((NX, LC, Q), bf16),
        pltpu.VMEM((NX, 8, Q), f32),
        pltpu.VMEM((LC + 32, NPAIR), f32),
        pltpu.VMEM((LC, NPAIR), bf16),
        pltpu.VMEM((8, NPAIR), f32),
        pltpu.VMEM((NX, LC, Q), bf16),
        pltpu.VMEM((NX, 8, Q), f32),
        pltpu.VMEM((NX * LM, NX * LM), f32),
        pltpu.VMEM((1, NX * LM), f32),
        pltpu.VMEM((NP, ROWS, 128), bf16),
        pltpu.VMEM((NP, ROWS, 128), bf16),
        pltpu.VMEM((ROWS, 128), bf16),
        pltpu.VMEM((NZ, ROWS, 128), bf16),
        pltpu.VMEM((16, 128), f32),
        pltpu.VMEM((NS, 16, 128), f32),
        dma((NZ // GROUP,)), dma((NZ // GROUP,)), dma, dma, dma, dma, dma, dma((NZ,)),
        dma((4,)), dma((4,)), dma, dma, dma, dma, dma, dma,
    ]
    vmem = pl.BlockSpec(memory_space=pltpu.VMEM)
    return pl.pallas_call(
        lambda *refs: kernel(factor, *refs),
        name="reduced_step",
        out_shape=(jax.ShapeDtypeStruct((LM, NX * LM), f32), jax.ShapeDtypeStruct((8, 128), f32)),
        in_specs=[vmem] * 6 + [pl.BlockSpec(memory_space=pltpu.SMEM)],
        out_specs=(vmem, vmem),
        scratch_shapes=scratch,
        compiler_params=pltpu.CompilerParams(
            collective_id=0, has_side_effects=True, vmem_limit_bytes=40 * 1024 * 1024
        ),
    )(*operands)


def body(reduced_coords, mode_basis, rest_shape, stiffness, send_slots, pair_peer, pair_slot, pair_count):
    local_modes, _, vertex_count = mode_basis.shape
    factor = local_modes * NX / (3.0 * vertex_count * NZ * NS)
    basis = jnp.transpose(mode_basis, (1, 0, 2)).reshape(LC, NV)
    hi = lax.reduce_precision(reduced_coords, 8, 7)
    mid = lax.reduce_precision(reduced_coords - hi, 8, 7)
    lo = reduced_coords - hi - mid
    parts = jnp.stack([hi, mid, lo])
    eye = jnp.concatenate([jnp.eye(3, dtype=f32), jnp.zeros((5, 3), f32)])
    coeff = (parts[:, None, None, :] * eye[None, :, :, None]).reshape(24, LC).astype(bf16)
    slots = send_slots.reshape(NZ, NS * NSLOT)
    ends = (pair_peer * NSLOT + pair_slot).reshape(2, NPAIR)
    hessian, gradient = step(
        factor, basis, coeff, rest_shape, stiffness.reshape(1, NV), slots, ends, pair_count
    )
    return hessian, gradient[0, :LM]


def solution(mesh):
    finer = Mesh(mesh.devices.reshape(NZ, 4, 2, NX), ("z", "y", "c", "x"))
    placed = (
        P("x"),
        P("x", None, VERTS),
        P(None, VERTS),
        P(VERTS),
        P(VERTS, None, None),
        P(VERTS, None, None),
        P(VERTS, None, None),
        P(VERTS),
    )
    return jax.shard_map(
        body, mesh=finer, in_specs=placed, out_specs=(P("x", None), P("x")), check_vma=False
    )
```

time: 261 us -> 93.9 us (0.36)
  Pallas kernels: 0 us -> 87.2 us
  local copies, waits for them, and re-layouts: 78.9 us -> 4.93 us
  waiting for transfers between devices: 65.8 us -> 0 us
  blocking collectives: 52.7 us -> 0 us
  starting transfers between devices: 42.9 us -> 0 us
  other arithmetic: 11.8 us -> 0.11 us
  matrix products: 6.41 us -> 0 us
    pallas_call x0 -> x1, Pallas kernels: none -> 87.2 us  [step(): pl.pallas_call(lambda *refs: kernel(factor, *refs), name='reduced_step',...]
    all_to_all x5 -> x0, waiting for transfers between devices: 65.8 us -> none  [the longest x1 29.8 us: body(): lax.all_to_all(outgoing_rows, VERTS, split_axis=2, concat_axis=2, tiled=T...]
    all_to_all x4 -> x0, blocking collectives: 52.7 us -> none  [the longest x2 24.5 us: sent_to_all(): lax.all_to_all(jnp.broadcast_to(x[None], (size, *x.shape)), axis, 0, 0, t...]
    gather x8 -> x0, local copies, waits for them, and re-layouts: 48 us -> none  [the longest x2 19.5 us: body(): jnp.take(incoming_rows.reshape(local_modes, 3, peer_count * slot_count),...]
    all_to_all x5 -> x0, starting transfers between devices: 42.9 us -> none  [the longest x1 20.5 us: body(): lax.all_to_all(outgoing_pos, VERTS, split_axis=1, concat_axis=1, tiled=True)]
    reshape x2 -> x1, local copies, waits for them, and re-layouts: 11.5 us -> 0.08 us  [body(): slots = send_slots.reshape(NZ, NS * NSLOT)]
    dot_general x4 -> x0, matrix products: 6.41 us -> none  [the longest x2 4.2 us: outer_sum(): lax.dot_general(left_rows, right_rows, (((1,), (1,)), ((), ())), preferre...]
    unnamed x57 -> x16, local copies, waits for them, and re-layouts: 10.3 us -> 4.24 us
  transfers between devices with their start and end apart: 5 -> 0, of which waited for: 3 -> 0; matrix products, arithmetic and copies ran while one was open for 29% -> 0% of each run, Pallas kernels for 0% -> 0%
where the time goes in v1:
time: 93.9 us; the launch traced here: 93.5 us
  Pallas kernels  87.2 us (93%)
  local copies, waits for them, and re-layouts  4.93 us (5%)
  between operations  1.35 us (1%)
    pallas_call x1, Pallas kernels, step(): pl.pallas_call(lambda *refs: kernel(factor, *refs), name='reduced_step',...  87.2 us
    unnamed x16, local copies, waits for them, and re-layouts  4.24 us

profile of v1, /device:TPU:1, one launch (start us, length us, event | category | flops | bytes accessed | tf_op | source)
XLA Modules:
  0.0 93.5 jit_solution(17233256614753926264)
XLA Ops:
  1.3 0.0 copy-start.6
  1.3 0.0 copy-start.4
  1.3 0.6 copy-done.6
  1.9 0.0 copy-start.3
  2.0 0.0 copy-done.4
  2.0 0.6 copy-done.3
  2.6 0.1 multiply_convert_fusion
  2.7 0.0 copy-start.5
  2.7 0.1 convert_element_type.7.refs_1_
  2.8 0.6 copy-done.5
  3.4 0.1 copy.11
  3.5 0.0 copy-start.1
  3.5 0.0 copy-start.2
  3.5 0.1 reshape.25.refs_4_
  3.6 0.6 copy-done.1
  4.2 0.0 copy-done.2
  4.2 0.0 copy-start
  4.2 1.0 %copy-done = bf16[64,3,1024]{2,0,1:T(8,128)(2,1)S(1)} copy-done((bf16[64,3,1024]{2,0,1:T(8,128)(2,1)S(1)}, bf16[64,3,1024]{2,0,1:T(8,128)(2,1)}, u32[]{:S(2)}) %copy-start) | copy-done | bytes 393240
  5.2 87.2 %reduced_step.1 = (f32[64,256]{1,0:T(8,128)S(1)}, f32[8,128]{1,0:T(8,128)S(1)}) custom-call(bf16[192,1024]{1,0:T(8,128)(2,1)S(1)} %bitcast.14, bf16[24,192]{1,0:T(8,128)(2,1)S(1)} %convert_element_type.7.refs_1_, f32[3,1024]{1,0:T(4,128)S(1)} %copy-done.1, f32[1,1024]{1,0:T(1,128)S(1)} %bitcast.15, s32[16,128]{1,0:T(8,128)S(1)} %reshape.25.refs_4_, ...), custom_call_target="tpu_custom_call" | custom-call | tf_op jit(solution)/shard_map/reduced_step/pallas_call | solution.py:355
  92.4 0.5 slice_bitcast_fusion
  92.9 0.6 copy.14
  (5 shorter events, 0.0 us)
Async XLA Ops:
  1.3 0.7 copy-start.6
  1.3 0.7 copy-start.4
  1.9 0.7 copy-start.3
  2.7 0.7 copy-start.5
  3.5 0.7 copy-start.1
  3.5 0.7 copy-start.2
  4.2 1.0 %copy-start = (bf16[64,3,1024]{2,0,1:T(8,128)(2,1)S(1)}, bf16[64,3,1024]{2,0,1:T(8,128)(2,1)}, u32[]{:S(2)}) copy-start(bf16[64,3,1024]{2,0,1:T(8,128)(2,1)} %param.9) | copy-start | bytes 1179652

commit v2 on v1

v2 whole, which is shorter than its diff:
```python
import jax
import jax.numpy as jnp
from jax import lax
from jax.experimental import pallas as pl
from jax.experimental.pallas import tpu as pltpu
from jax.sharding import Mesh
from jax.sharding import PartitionSpec as P

VERTS = ("z", "y", "c")
MESH = pl.DeviceIdType.MESH
NZ, NS, NX = 16, 8, 4
NP = NX * NS
LM, LC = 64, 192
NV, NPAIR, NSLOT = 1024, 1024, 16
Q = 256
ROWS = 24
GROUP = 4
SPANS = ((0, 1), (1, 2), (3, 4), (7, 9))
EARLY = 9
f32, bf16 = jnp.float32, jnp.bfloat16

barrier_reach = 1.5
gap_offset = 0.1


def split3(v):
    hi = v.astype(bf16).astype(f32)
    mid = (v - hi).astype(bf16).astype(f32)
    return hi, mid, v - hi - mid


def dot_nt(a, b):
    return lax.dot_general(a, b, (((1,), (1,)), ((), ())), preferred_element_type=f32)


def dot_nn(a, b):
    return lax.dot_general(a, b, (((1,), (0,)), ((), ())), preferred_element_type=f32)


def offset_of(n):
    m = (n + 1) // 2
    odd = m % 2
    hops = odd * ((m + 1) // 2) + (1 - odd) * (8 - m // 2)
    return ((n % 2) * hops + (1 - n % 2) * (NZ - hops)) * (1 - n // (NZ - 1))


def barrier_slopes(distance):
    excess = distance - barrier_reach
    ratio_log = jnp.log(distance / barrier_reach)
    slope_term = -(2.0 * excess * ratio_log + excess * excess / distance)
    curvature = -(2.0 * ratio_log + 4.0 * excess / distance - excess * excess / (distance * distance))
    inside = distance < barrier_reach
    return jnp.where(inside, slope_term, 0.0), jnp.where(inside, curvature, 0.0)


def accumulate(parts, s, scale, bend, hess, grad, exact):
    lever = jnp.zeros((NX * LM, Q), f32)
    total = None
    slopes = None
    for k in range(3):
        x = parts[k].astype(f32)
        xb = x.astype(bf16)
        sk = s[k : k + 1, :]
        lever = lever + x * sk
        part = dot_nt((x * scale).astype(bf16), xb)
        total = part if total is None else total + part
        hi, mid, lo = split3(scale * sk)
        force = jnp.concatenate([hi, mid, lo, jnp.zeros((13, Q), f32)], axis=0).astype(bf16)
        gpart = dot_nt(force, xb)
        if not exact:
            gpart = gpart + dot_nt(force, (x - xb.astype(f32)).astype(bf16))
        slopes = gpart if slopes is None else slopes + gpart
    total = total + dot_nt((lever * bend).astype(bf16), lever.astype(bf16))
    slopes = jnp.sum(slopes, axis=0, keepdims=True)
    if exact:
        hess[...] = total
        grad[...] = slopes
    else:
        hess[...] = hess[...] + total
        grad[...] = grad[...] + slopes


def kernel(
    factor,
    basis_hbm, coord_hbm, rest_hbm, stiff_hbm, slots_hbm, peer_hbm, seat_hbm, count_hbm,
    out_h, out_g,
    wide, coord, rest_v, stiff, slots, peer, seat, count,
    obuf, stage, rows_in, restg, restp, resta, restz,
    part_s, xb, xp, ends, acc, early_s, early_r, late_s, late_r, usend, xu,
    hess, grad, hsend, hplane, zsend, hz, csend, hc,
    in_sem, p1_s, p1_r, ri_s, ri_r, rz_s, rz_r, zm_s, zm_r,
    x_s, x_r, a_s, a_r, b_s, b_r, c_s, c_r,
):
    z, y, c, x = (lax.axis_index(n) for n in ("z", "y", "c", "x"))
    s = y * 2 + c
    p = x * NS + s

    def plane_peer(k):
        q = lax.rem(p + k, NP)
        sq = lax.rem(q, NS)
        return q, {"x": q // NS, "y": sq // 2, "c": lax.rem(sq, 2)}

    def near_peer(k):
        q = lax.rem(s + k, NS)
        return q, {"y": q // 2, "c": lax.rem(q, 2)}

    def remote(src, dst, ssem, rsem, where):
        return pltpu.make_async_remote_copy(src, dst, ssem, rsem, device_id=where, device_id_type=MESH)

    def arrived(ref, sem):
        remote(ref, ref, c_s, sem, {"z": z}).wait_recv()

    def left(ref, sem):
        remote(ref, ref, sem, c_r, {"z": z}).wait_send()

    bar = pltpu.get_barrier_semaphore()

    @pl.loop(1, NZ)
    def _(k):
        pl.semaphore_signal(bar, inc=1, device_id={"z": lax.rem(z + k, NZ)}, device_id_type=MESH)

    @pl.loop(1, NP)
    def _(k):
        pl.semaphore_signal(bar, inc=1, device_id=plane_peer(k)[1], device_id_type=MESH)

    loads = [
        pltpu.make_async_copy(src, dst, in_sem.at[i])
        for i, (src, dst) in enumerate(
            (
                (slots_hbm, slots), (basis_hbm, wide.at[pl.ds(0, LC)]), (rest_hbm, rest_v), (coord_hbm, coord),
                (stiff_hbm, stiff), (peer_hbm, peer), (seat_hbm, seat), (count_hbm, count),
            )
        )
    ]
    for load in loads:
        load.start()
    wide[LC:Q, :] = jnp.zeros((Q - LC, NV), bf16)
    for load in loads:
        load.wait()

    rest = rest_v[...]
    mine = jnp.where(x == 0, rest[0:1], jnp.where(x == 1, rest[1:2], jnp.where(x == 2, rest[2:3], 0.0)))
    hi, mid, lo = split3(mine)
    rest_rows = jnp.concatenate([hi, mid, lo, jnp.zeros((13, NV), f32)], axis=0).astype(bf16)
    lane = lax.broadcasted_iota(jnp.int32, (128, 128), 1)
    seat_of = lax.broadcasted_iota(jnp.int32, (128, 128), 0) // NSLOT
    listed = jnp.concatenate([slots[...].astype(f32)] * NS, axis=0)
    lanef = lane.astype(f32)

    @pl.loop(0, NZ // GROUP)
    def _(g):
        hots = []
        for i in range(GROUP):
            zq = lax.rem(z + offset_of(g * GROUP + i), NZ)
            col = jnp.sum(jnp.where(lane == seat_of + zq * NS, listed, 0.0), axis=1, keepdims=True)
            blocks = [jnp.where(col == lanef + 128.0 * b, 1.0, 0.0).astype(bf16) for b in range(NV // 128)]
            hots.append(jnp.concatenate(blocks, axis=1))
        hot = jnp.concatenate(hots, axis=0)
        picked = dot_nt(hot, wide[...])
        tail = picked[:, 128:256]
        turned = pltpu.roll(tail, 64, 1)
        tail = tail.reshape(GROUP * NS, 2, 8, 128)[:, 0] + turned.reshape(GROUP * NS, 2, 8, 128)[:, 1]
        chunk = jnp.concatenate([picked[:, 0:128].reshape(GROUP * NS, 16, 128), tail], axis=1)
        chunk = chunk.astype(bf16).reshape(GROUP, NS, ROWS, 128)
        rests = jnp.sum(dot_nt(rest_rows, hot), axis=0, keepdims=True)
        for i in range(GROUP):
            n = g * GROUP + i
            obuf[:, pl.ds(n, 1)] = chunk[i][:, None]
            restg[pl.ds(n, 1), :] = rests[:, 128 * i : 128 * (i + 1)]

    line = jnp.concatenate([coord[...]] * 3 + [jnp.zeros((1, Q - LC), f32)], axis=1)
    own_row = lax.broadcasted_iota(jnp.int32, (8, Q), 0) == lax.broadcasted_iota(jnp.int32, (8, Q), 1) // LM
    hi, mid, lo = split3(jnp.where(own_row, line, 0.0))
    coeff = jnp.concatenate([hi, mid, lo, jnp.zeros((8, Q), f32)], axis=0).astype(bf16)

    moved = dot_nn(coeff, wide[...])
    part_s[...] = moved[0:8] + moved[8:16] + moved[16:24]

    pl.semaphore_wait(bar, NZ - 1 + NP - 1)

    for g, (start, size) in enumerate(SPANS):

        @pl.loop(1, NS)
        def _(k):
            q, where = near_peer(k)
            span = pl.ds(start, size)
            remote(obuf.at[q, span], stage.at[span, s], p1_s.at[g], p1_r.at[g], where).start()

        if g == 0:

            @pl.loop(1, NS)
            def _(k):
                remote(restg, restp.at[s], ri_s, ri_r, near_peer(k)[1]).start()

    @pl.loop(1, NX)
    def _(k):
        q = lax.rem(x + k, NX)
        cols = pl.ds(pl.multiple_of(q * Q, Q), Q)
        remote(wide.at[pl.ds(0, LC), cols], xb.at[x], x_s.at[0], x_r.at[0], {"x": q}).start()
        remote(part_s.at[:, cols], xp.at[x], x_s.at[1], x_r.at[1], {"x": q}).start()

    own = pl.ds(pl.multiple_of(x * Q, Q), Q)
    stage[:, pl.ds(s, 1)] = obuf[s][:, None]
    restp[s] = restg[...]
    xb[x] = wide[0:LC, own]
    xp[x] = part_s[:, own]

    def toward(n):
        return {"z": lax.rem(z + offset_of(n), NZ)}

    for g, (start, size) in enumerate(SPANS):
        arrived(obuf.at[pl.ds(0, NS - 1), pl.ds(0, size)], p1_r.at[g])
        for n in range(start, min(start + size, NZ - 1)):
            remote(stage.at[n], rows_in.at[n], zm_s, zm_r.at[n], toward(n)).start()
        if g == 0:
            arrived(restp.at[pl.ds(0, NS - 1)], ri_r)
            place_of = lax.broadcasted_iota(jnp.int32, (NZ, 128), 1) // NSLOT
            gathered = jnp.zeros((NZ, 128), f32)
            for q in range(NS):
                shift = lax.rem((q - s + NS) * NSLOT, 128)
                gathered = jnp.where(place_of == q, pltpu.roll(restp[q], shift, 1), gathered)
            resta[...] = gathered.reshape(NZ, 1, 128)
            for n in range(NZ - 1):
                remote(resta.at[n], restz.at[n], rz_s, rz_r, toward(n)).start()
            restz[NZ - 1] = resta[NZ - 1]
    rows_in[NZ - 1] = stage[NZ - 1]

    for i, buf in enumerate((xb, xp)):
        arrived(buf.at[pl.ds(0, NX - 1)], x_r.at[i])
    disp = xp[0] + xp[1] + xp[2] + xp[3]
    square = 1.0 + disp[0:1] * disp[0:1] + disp[1:2] * disp[1:2] + disp[2:3] * disp[2:3]
    rate = stiff[:, own] / jnp.sqrt(square)
    columns = [xb[:, LM * k : LM * (k + 1), :].reshape(NX * LM, Q) for k in range(3)]
    accumulate(columns, disp, rate, -rate / square, hess, grad, True)

    acc[...] = jnp.zeros_like(acc)
    pick = lax.broadcasted_iota(jnp.int32, (8, 128), 0) == x
    code = lax.broadcasted_iota(jnp.int32, (128, NPAIR), 0)
    ends[...] = peer[...] * NSLOT + seat[...]
    arrived(resta.at[pl.ds(0, NZ - 1)], rz_r)

    def consume(n, awaited=True):
        base = lax.rem(z + NZ - offset_of(n), NZ) * 128
        first = jnp.where(ends[0:1, :] - base == code, 1.0, 0.0)
        second = jnp.where(ends[1:2, :] - base == code, 1.0, 0.0)
        choose = (first - second).astype(bf16)
        if awaited:
            arrived(stage.at[n], zm_r.at[n])
        got = rows_in[n].astype(f32)
        head = got[:, 0:16].reshape(128, 128)
        tail = got[:, 16:24]
        turned = pltpu.roll(tail.reshape(64, 128), 64, 1).reshape(NS, 1, 8, 128)
        tail = jnp.concatenate([tail.reshape(NS, 1, 8, 128), turned], axis=1).reshape(128, 128)
        cols = jnp.concatenate([jnp.transpose(head), jnp.transpose(tail)[0:LM]], axis=0).astype(bf16)
        pos = dot_nn(coeff[:, 0:LC], cols)
        pos = pos[0:8] + pos[8:16] + pos[16:24] + jnp.where(pick, restz[n], 0.0)
        hi, mid, lo = split3(pos)
        pos = jnp.concatenate([hi, mid, lo, jnp.zeros((8, 128), f32)], axis=0).astype(bf16)
        acc[...] = acc[...] + dot_nn(jnp.concatenate([cols, pos], axis=0), choose)

    def hand_out(src, dst, i):
        @pl.loop(1, NX)
        def _(k):
            q = lax.rem(x + k, NX)
            cols = pl.ds(pl.multiple_of(q * Q, Q), Q)
            remote(src.at[:, cols], dst.at[x], x_s.at[i], x_r.at[i], {"x": q}).start()

        dst[x] = src[:, own]

    consume(NZ - 1, False)

    @pl.loop(0, EARLY)
    def _(n):
        consume(n)

    diff = acc[0:LC, :]
    high = diff.astype(bf16)
    early_s[0:LC, :] = high
    early_s[LC : 2 * LC, :] = (diff - high.astype(f32)).astype(bf16)
    hand_out(early_s, early_r, 4)
    acc[0:LC, :] = jnp.zeros((LC, NPAIR), f32)

    @pl.loop(EARLY, NZ - 1)
    def _(n):
        consume(n)

    usend[...] = acc[LC : LC + 8, :] + acc[LC + 8 : LC + 16, :] + acc[LC + 16 : LC + 24, :]
    hand_out(usend, xu, 3)
    late_s[...] = acc[0:LC, :].astype(bf16)
    hand_out(late_s, late_r, 2)
    arrived(xu.at[pl.ds(0, NX - 1)], x_r.at[3])
    gap = xu[0] + xu[1] + xu[2] + xu[3]
    distance = gap[0:1] * gap[0:1] + gap[1:2] * gap[1:2] + gap[2:3] * gap[2:3] + gap_offset
    slope, bend = barrier_slopes(distance)
    live = lax.broadcasted_iota(jnp.int32, (1, Q), 1) + x * Q < count[...]
    slope = jnp.where(live, slope, 0.0)
    bend = jnp.where(live, bend, 0.0)
    arrived(early_r.at[pl.ds(0, NX - 1)], x_r.at[4])
    known = early_r[:, 0:LC].astype(f32) + early_r[:, LC : 2 * LC].astype(f32)
    arrived(late_r.at[pl.ds(0, NX - 1)], x_r.at[2])
    known = known + late_r[...].astype(f32)
    columns = [known[:, LM * k : LM * (k + 1)].reshape(NX * LM, Q) for k in range(3)]
    accumulate(columns, gap, 2.0 * slope, 4.0 * bend, hess, grad, False)

    def packed_grad(row):
        hi = row.astype(bf16).astype(f32)
        lo = row - hi
        return jnp.concatenate(
            [hi[:, 0:128], hi[:, 128:256], lo[:, 0:128], lo[:, 128:256], jnp.zeros((4, 128), f32)], axis=0
        )

    h = hess[...]
    tail = jnp.broadcast_to(packed_grad(grad[...])[None], (NP, 8, 128))
    hsend[...] = jnp.concatenate(
        [h[:, 0:128].reshape(NP, 8, 128), h[:, 128:256].reshape(NP, 8, 128), tail], axis=1
    ).astype(bf16)

    @pl.loop(1, NP)
    def _(k):
        q, where = plane_peer(k)
        remote(hsend.at[q], hplane.at[p], a_s, a_r, where).start()

    hplane[p] = hsend[p]
    arrived(hsend.at[pl.ds(0, NP - 1)], a_r)
    total = jnp.sum(hplane[...].astype(f32), axis=0)
    g0, g1 = total[16:17] + total[18:19], total[17:18] + total[19:20]
    zsend[...] = jnp.concatenate([total[0:16], packed_grad(jnp.concatenate([g0, g1], axis=1))], axis=0).astype(bf16)

    @pl.loop(1, NZ)
    def _(k):
        remote(zsend, hz.at[z], b_s, b_r, {"z": lax.rem(z + k, NZ)}).start()

    hz[z] = zsend[...]
    arrived(hz.at[pl.ds(0, NZ - 1)], b_r)
    total = jnp.sum(hz[...].astype(f32), axis=0) * factor
    csend[...] = total[0:16]

    @pl.loop(1, NS)
    def _(k):
        remote(csend, hc.at[s], c_s, c_r, near_peer(k)[1]).start()

    hc[s] = csend[...]
    g0, g1 = total[16:17] + total[18:19], total[17:18] + total[19:20]
    half = jnp.broadcast_to(jnp.where(x >= 2, g1, g0), (8, 128))
    half = jnp.where(lax.rem(x, 2) == 1, pltpu.roll(half, 64, 1), half)
    out_g[...] = half[0:1, 0:LM]

    for g, (_start, size) in enumerate(SPANS):
        left(obuf.at[pl.ds(0, NS - 1), pl.ds(0, size)], p1_s.at[g])
    for src, sem in (
        (restp.at[pl.ds(0, NS - 1)], ri_s),
        (resta.at[pl.ds(0, NZ - 1)], rz_s),
        (stage.at[pl.ds(0, NZ - 1)], zm_s),
        (xb.at[pl.ds(0, NX - 1)], x_s.at[0]),
        (xp.at[pl.ds(0, NX - 1)], x_s.at[1]),
        (late_r.at[pl.ds(0, NX - 1)], x_s.at[2]),
        (xu.at[pl.ds(0, NX - 1)], x_s.at[3]),
        (early_r.at[pl.ds(0, NX - 1)], x_s.at[4]),
        (hsend.at[pl.ds(0, NP - 1)], a_s),
        (hz.at[pl.ds(0, NZ - 1)], b_s),
        (hc.at[pl.ds(0, NS - 1)], c_s),
    ):
        left(src, sem)

    arrived(hc.at[pl.ds(0, NS - 1)], c_r)
    out_h[:, 0:128] = hc[:, 0:8, :].reshape(LM, 128)
    out_h[:, 128:256] = hc[:, 8:16, :].reshape(LM, 128)


def step(factor, *operands):
    dma = pltpu.SemaphoreType.DMA
    i32 = jnp.int32
    scratch = [
        pltpu.VMEM((Q, NV), bf16),
        pltpu.VMEM((1, LM), f32),
        pltpu.VMEM((3, NV), f32),
        pltpu.VMEM((1, NV), f32),
        pltpu.VMEM((NSLOT, NZ * NS), i32),
        pltpu.VMEM((2, NPAIR), i32),
        pltpu.VMEM((2, NPAIR), i32),
        pltpu.VMEM((1, 1), i32),
        pltpu.VMEM((NS, NZ, ROWS, 128), bf16),
        pltpu.VMEM((NZ, NS, ROWS, 128), bf16),
        pltpu.VMEM((NZ, NS, ROWS, 128), bf16),
        pltpu.VMEM((NZ, 128), f32),
        pltpu.VMEM((NS, NZ, 128), f32),
        pltpu.VMEM((NZ, 1, 128), f32),
        pltpu.VMEM((NZ, 1, 128), f32),
        pltpu.VMEM((8, NV), f32),
        pltpu.VMEM((NX, LC, Q), bf16),
        pltpu.VMEM((NX, 8, Q), f32),
        pltpu.VMEM((2, NPAIR), i32),
        pltpu.VMEM((LC + 32, NPAIR), f32),
        pltpu.VMEM((2 * LC, NPAIR), bf16),
        pltpu.VMEM((NX, 2 * LC, Q), bf16),
        pltpu.VMEM((LC, NPAIR), bf16),
        pltpu.VMEM((NX, LC, Q), bf16),
        pltpu.VMEM((8, NPAIR), f32),
        pltpu.VMEM((NX, 8, Q), f32),
        pltpu.VMEM((NX * LM, NX * LM), f32),
        pltpu.VMEM((1, NX * LM), f32),
        pltpu.VMEM((NP, ROWS, 128), bf16),
        pltpu.VMEM((NP, ROWS, 128), bf16),
        pltpu.VMEM((ROWS, 128), bf16),
        pltpu.VMEM((NZ, ROWS, 128), bf16),
        pltpu.VMEM((16, 128), f32),
        pltpu.VMEM((NS, 16, 128), f32),
        dma((8,)), dma((len(SPANS),)), dma((len(SPANS),)), dma, dma, dma, dma, dma, dma((NZ,)),
        dma((5,)), dma((5,)), dma, dma, dma, dma, dma, dma,
    ]
    vmem = pl.BlockSpec(memory_space=pltpu.VMEM)
    return pl.pallas_call(
        lambda *refs: kernel(factor, *refs),
        name="reduced_step",
        out_shape=(jax.ShapeDtypeStruct((LM, NX * LM), f32), jax.ShapeDtypeStruct((1, LM), f32)),
        in_specs=[pl.BlockSpec(memory_space=pltpu.HBM)] * 8,
        out_specs=(vmem, vmem),
        scratch_shapes=scratch,
        compiler_params=pltpu.CompilerParams(
            collective_id=0, has_side_effects=True, vmem_limit_bytes=56 * 1024 * 1024
        ),
    )(*operands)


def body(reduced_coords, mode_basis, rest_shape, stiffness, send_slots, pair_peer, pair_slot, pair_count):
    local_modes, _, vertex_count = mode_basis.shape
    factor = local_modes * NX / (3.0 * vertex_count * NZ * NS)
    hessian, gradient = step(
        factor,
        jnp.transpose(mode_basis, (1, 0, 2)).reshape(LC, NV),
        reduced_coords.reshape(1, LM),
        rest_shape,
        stiffness.reshape(1, NV),
        jnp.transpose(send_slots[0]),
        pair_peer[0],
        pair_slot[0],
        pair_count.reshape(1, 1),
    )
    return hessian, gradient.reshape(LM)


def solution(mesh):
    finer = Mesh(mesh.devices.reshape(NZ, 4, 2, NX), ("z", "y", "c", "x"))
    placed = (
        P("x"),
        P("x", None, VERTS),
        P(None, VERTS),
        P(VERTS),
        P(VERTS, None, None),
        P(VERTS, None, None),
        P(VERTS, None, None),
        P(VERTS),
    )
    return jax.shard_map(
        body, mesh=finer, in_specs=placed, out_specs=(P("x", None), P("x")), check_vma=False
    )
```

time: 93.9 us -> 90.2 us (0.961)
  local copies, waits for them, and re-layouts: 4.93 us -> 1.99 us
    unnamed x16 -> x4, local copies, waits for them, and re-layouts: 4.24 us -> 1.99 us
where the time goes in v2:
time: 90.2 us; the launch traced here: 89.9 us
  Pallas kernels  86.6 us (96%)
  local copies, waits for them, and re-layouts  1.99 us (2%)
  between operations  1.3 us (1%)
    pallas_call x1, Pallas kernels, step(): pl.pallas_call(lambda *refs: kernel(factor, *refs), name='reduced_step',...  86.6 us
    unnamed x4, local copies, waits for them, and re-layouts  1.99 us

profile of v2, /device:TPU:1, one launch (start us, length us, event | category | flops | bytes accessed | tf_op | source)
XLA Modules:
  0.0 89.9 jit_solution(14800554003722916301)
XLA Ops:
  1.3 86.6 %reduced_step.1 = (f32[64,256]{1,0:T(8,128)}, f32[1,64]{1,0:T(1,128)}) custom-call(bf16[192,1024]{1,0:T(8,128)(2,1)} %bitcast.13, f32[1,64]{1,0:T(1,128)} %bitcast.18, f32[3,1024]{1,0:T(4,128)} %refs_2_.1, f32[1,1024]{1,0:T(1,128)} %bitcast.17, s32[16,128]{1,0:T(8,128)} %bitcast.14, s32[2,1024]{1,0:T(2,128)} %bitcast.15, s32[2,1024]{1,0:T(2,128)} %bitcast.16, ...), custom_call_target="tpu_custom_call" | custom-call | tf_op jit(solution)/shard_map/reduced_step/pallas_call | solution.py:412
  87.9 0.0 copy-start
  87.9 1.5 %copy.13 = f32[64,256]{1,0:T(8,128)} copy(f32[64,256]{1,0:T(8,128)} %get-tuple-element.8) | data formatting | bytes 131072
  89.4 0.0 copy-done
  89.4 0.5 copy.14
Async XLA Ops:
  87.9 1.5 %copy-start = (f32[1,64]{1,0:T(1,128)S(1)}, f32[1,64]{1,0:T(1,128)}, u32[]{:S(2)}) copy-start(f32[1,64]{1,0:T(1,128)} %get-tuple-element.5) | copy-start | bytes 772

commit v3 on v2

--- a/solution.py
+++ b/solution.py
@@ -15,7 +15,7 @@
 Q = 256
 ROWS = 24
 GROUP = 4
-SPANS = ((0, 1), (1, 2), (3, 4), (7, 9))
+SPANS = ((1, 2), (3, 4), (7, 9))
 EARLY = 9
 f32, bf16 = jnp.float32, jnp.bfloat16
 
@@ -104,6 +104,10 @@
         q = lax.rem(s + k, NS)
         return q, {"y": q // 2, "c": lax.rem(q, 2)}
 
+    def far_peer(k):
+        q, where = near_peer(k)
+        return q, {"z": lax.rem(z + offset_of(0), NZ), **where}
+
     def remote(src, dst, ssem, rsem, where):
         return pltpu.make_async_remote_copy(src, dst, ssem, rsem, device_id=where, device_id_type=MESH)
 
@@ -118,6 +122,10 @@
     @pl.loop(1, NZ)
     def _(k):
         pl.semaphore_signal(bar, inc=1, device_id={"z": lax.rem(z + k, NZ)}, device_id_type=MESH)
+
+    @pl.loop(1, NS)
+    def _(k):
+        pl.semaphore_signal(bar, inc=1, device_id=far_peer(k)[1], device_id_type=MESH)
 
     @pl.loop(1, NP)
     def _(k):
@@ -176,7 +184,12 @@
     moved = dot_nn(coeff, wide[...])
     part_s[...] = moved[0:8] + moved[8:16] + moved[16:24]
 
-    pl.semaphore_wait(bar, NZ - 1 + NP - 1)
+    pl.semaphore_wait(bar, NZ - 1 + NP - 1 + NS - 1)
+
+    @pl.loop(0, NS)
+    def _(k):
+        q, where = far_peer(k)
+        remote(obuf.at[q, 0], rows_in.at[0, s], zm_s, zm_r.at[0], where).start()
 
     for g, (start, size) in enumerate(SPANS):
 
@@ -292,7 +305,7 @@
     gap = xu[0] + xu[1] + xu[2] + xu[3]
     distance = gap[0:1] * gap[0:1] + gap[1:2] * gap[1:2] + gap[2:3] * gap[2:3] + gap_offset
     slope, bend = barrier_slopes(distance)
-    live = lax.broadcasted_iota(jnp.int32, (1, Q), 1) + x * Q < count[...]
+    live = lax.broadcasted_iota(jnp.int32, (1, Q), 1) + x * Q < count[0]
     slope = jnp.where(live, slope, 0.0)
     bend = jnp.where(live, bend, 0.0)
     arrived(early_r.at[pl.ds(0, NX - 1)], x_r.at[4])
@@ -378,7 +391,7 @@
         pltpu.VMEM((NSLOT, NZ * NS), i32),
         pltpu.VMEM((2, NPAIR), i32),
         pltpu.VMEM((2, NPAIR), i32),
-        pltpu.VMEM((1, 1), i32),
+        pltpu.SMEM((1,), i32),
         pltpu.VMEM((NS, NZ, ROWS, 128), bf16),
         pltpu.VMEM((NZ, NS, ROWS, 128), bf16),
         pltpu.VMEM((NZ, NS, ROWS, 128), bf16),
@@ -434,7 +447,7 @@
         jnp.transpose(send_slots[0]),
         pair_peer[0],
         pair_slot[0],
-        pair_count.reshape(1, 1),
+        pair_count,
     )
     return hessian, gradient.reshape(LM)
 

time: 90.2 us -> 89.9 us (level)
  no operation moved by 1% of the time
where the time goes in v3:
time: 89.9 us; the launch traced here: 89.7 us
  Pallas kernels  86.4 us (96%)
  local copies, waits for them, and re-layouts  1.99 us (2%)
  between operations  1.3 us (1%)
    pallas_call x1, Pallas kernels, step(): pl.pallas_call(lambda *refs: kernel(factor, *refs), name='reduced_step',...  86.4 us
    unnamed x4, local copies, waits for them, and re-layouts  1.99 us

profile of v3, /device:TPU:1, one launch (start us, length us, event | category | flops | bytes accessed | tf_op | source)
XLA Modules:
  0.0 89.7 jit_solution(14057089831089373145)
XLA Ops:
  1.3 86.4 %reduced_step.1 = (f32[64,256]{1,0:T(8,128)}, f32[1,64]{1,0:T(1,128)}) custom-call(bf16[192,1024]{1,0:T(8,128)(2,1)} %bitcast.11, f32[1,64]{1,0:T(1,128)} %bitcast.16, f32[3,1024]{1,0:T(4,128)} %refs_2_.1, f32[1,1024]{1,0:T(1,128)} %bitcast.15, s32[16,128]{1,0:T(8,128)} %bitcast.12, s32[2,1024]{1,0:T(2,128)} %bitcast.13, s32[2,1024]{1,0:T(2,128)} %bitcast.14, ...), custom_call_target="tpu_custom_call" | custom-call | tf_op jit(solution)/shard_map/reduced_step/pallas_call | solution.py:425
  87.7 0.0 copy-start
  87.7 1.5 %copy.13 = f32[64,256]{1,0:T(8,128)} copy(f32[64,256]{1,0:T(8,128)} %get-tuple-element.8) | data formatting | bytes 131072
  89.2 0.0 copy-done
  89.2 0.5 copy.14
Async XLA Ops:
  87.7 1.5 %copy-start = (f32[1,64]{1,0:T(1,128)S(1)}, f32[1,64]{1,0:T(1,128)}, u32[]{:S(2)}) copy-start(f32[1,64]{1,0:T(1,128)} %get-tuple-element.5) | copy-start | bytes 772
